TPU v7x, 256 devices: a whole 4x4x8 slice. The times are simulated.
256 devices in a mesh: dp: 4 (over y), expert: 64 (over z, x, core).
Axes of the slice: x: 4, y: 4, z: 8, core: 2. Of those that a mesh axis runs over, the one named last changes fastest.
Arguments:
- tokens: bfloat16 [131072, 2048], P(('dp', 'expert')), may hold values from -6 to 6
- expert_ids: int32 [131072, 1], P(('dp', 'expert')), may hold values from 0 to 63; in each aligned block of 512 rows (0 to 511, 512 to 1023, ...) at most 16 rows name the same one
- gate_proj: bfloat16 [64, 2048, 768], P('expert'), may hold values from -0.125 to 0.125
- up_proj: bfloat16 [64, 2048, 768], P('expert'), may hold values from -0.125 to 0.125
- down_proj: bfloat16 [64, 768, 2048], P('expert'), may hold values from -0.21875 to 0.21875
Outputs:
- mixed: bfloat16 [131072, 2048], P(('dp', 'expert'))
- slot_index: int32 [131072], P(('dp', 'expert'))
Inputs may be any that keep to these rules, and one draw needn't show every extreme that they name: `expert_ids`: among the rows of one device no expert is named more than 16 times; in some devices' rows one expert is named exactly 16 times.
All inputs are finite; a program needn't handle non-finite values.
Results may differ from a plain program's by a relative error of at most 0.0046.
The roundings to bfloat16 on the way count: a program that leaves them out, or rounds other values in their place, can miss the bound.
Values may be sent and summed in bfloat16 or wider, within the bound.
A program may use at most 64 MiB of HBM per device.

v0:
```python
import jax
import jax.numpy as jnp
from jax import lax
from jax.sharding import PartitionSpec as P


def copy_for_each(array, axis):
    copies = jnp.broadcast_to(array, (lax.axis_size(axis), *array.shape))
    return lax.all_to_all(copies, axis, split_axis=0, concat_axis=0, tiled=True)


def joined_by_halves(pieces, combine):
    while len(jax.tree.leaves(pieces)[0]) > 1:
        pieces = jax.vmap(combine)(*(pieces[side::2] for side in (0, 1)))
    return pieces[0]


def prefix(array, axis, combine, identity):
    size, index = (lax.axis_size(axis), lax.axis_index(axis))
    passed = jnp.arange(size) < index

    def kept(part, zero, own):
        part = jnp.where(
            passed.reshape(-1, *(1 for _ in own.shape)), part, jnp.asarray(zero, own.dtype)
        )
        return part

    pieces = copy_for_each(array, axis)
    return joined_by_halves(kept(pieces, identity, array), combine)


def of_everyone(array, axis):
    return copy_for_each(array, axis).sum(axis=0)


def add_counts(earlier, later):
    return earlier + later


def expert_ffn(rows, gate_proj, up_proj, down_proj):
    gate_val = jnp.dot(rows, gate_proj[0], preferred_element_type=jnp.float32)
    up_val = jnp.dot(rows, up_proj[0], preferred_element_type=jnp.float32)
    hidden = (jax.nn.silu(gate_val) * up_val).astype(jnp.bfloat16)
    return jnp.dot(hidden, down_proj[0], preferred_element_type=jnp.float32).astype(jnp.bfloat16)


def on_device(tokens, expert_ids, gate_proj, up_proj, down_proj):
    tok_rows, width = tokens.shape
    experts_all = lax.axis_size("expert")
    most = 2 * tok_rows // experts_all
    capacity = tok_rows * lax.axis_size("dp")
    choices = expert_ids[:, 0]
    onehot = (choices[:, None] == jnp.arange(experts_all, dtype=jnp.int32)[None, :]).astype(
        jnp.int32
    )
    counts = jnp.sum(onehot, axis=0)
    inner = prefix(counts, "expert", add_counts, jnp.zeros_like(counts))
    totals = of_everyone(counts, "expert")
    outer = prefix(totals, "dp", add_counts, jnp.zeros_like(totals))
    offset = inner + outer
    before = jnp.cumsum(onehot, axis=0) - onehot
    local_rank = jnp.sum(before * onehot, axis=1)
    global_slot = (jnp.sum(onehot * offset[None, :], axis=1) + local_rank).astype(jnp.int32)
    is_kept = global_slot < capacity
    position = choices * most + local_rank
    targets = jnp.arange(experts_all * most, dtype=jnp.int32)
    dispatch = ((targets[:, None] == position[None, :]) & is_kept[None, :]).astype(jnp.bfloat16)
    outgoing = jnp.dot(dispatch, tokens, preferred_element_type=jnp.float32).astype(jnp.bfloat16)
    outgoing = outgoing.reshape(experts_all, most, width)
    arrived = lax.all_to_all(outgoing, "expert", split_axis=0, concat_axis=0, tiled=True)
    sources, slots_here, _ = arrived.shape
    flat = arrived.reshape(sources * slots_here, width)
    returned = lax.all_to_all(
        expert_ffn(flat, gate_proj, up_proj, down_proj).reshape(sources, slots_here, width),
        "expert",
        split_axis=0,
        concat_axis=0,
        tiled=True,
    )
    flat_back = returned.reshape(experts_all * most, width)
    mixed = lax.dot_general(
        dispatch, flat_back, (((0,), (0,)), ((), ())), preferred_element_type=jnp.float32
    )
    return (mixed.astype(jnp.bfloat16), global_slot)


def solution(mesh):
    in_specs = (
        P(("dp", "expert"), None),
        P(("dp", "expert"), None),
        P("expert", None, None),
        P("expert", None, None),
        P("expert", None, None),
    )
    out_specs = (P(("dp", "expert"), None), P(("dp", "expert")))
    return jax.shard_map(
        on_device, mesh=mesh, in_specs=in_specs, out_specs=out_specs, check_vma=False
    )
```

profile of v0, /device:TPU:99, one launch (start us, length us, event | category | flops | bytes accessed | tf_op | source)
XLA Modules:
  0.0 261.4 jit_solution(8329662366892537116)
XLA Ops:
  0.6 0.0 copy-start
  0.6 0.9 convert_reduce_fusion
  1.6 0.6 broadcast_in_dim.37
  2.2 11.0 %all-to-all-start = ((s32[64,1,64]{2,1,0:T(1,128)}), s32[64,1,64]{2,1,0:T(1,128)S(1)}, u32[]{:S(2)}, u32[]{:S(2)}) async-start(s32[64,1,64]{2,1,0:T(1,128)} %broadcast_in_dim.37), calls=%async_computation | async-start | bytes 65536 | tf_op jit(solution)/shard_map/all_to_all | solution.py:9
  13.3 0.7 fusion.18
  14.0 1.2 reduce-window.6
  15.2 0.2 slice_reduce_fusion
  15.5 3.5 %all-to-all-done = s32[64,1,64]{2,1,0:T(1,128)S(1)} async-done(((s32[64,1,64]{2,1,0:T(1,128)}), s32[64,1,64]{2,1,0:T(1,128)S(1)}, u32[]{:S(2)}, u32[]{:S(2)}) %all-to-all-start) | async-done | bytes 16416 | tf_op jit(solution)/shard_map/all_to_all | solution.py:9
  18.9 0.1 reduce_sum.38
  19.0 0.6 broadcast_in_dim.40
  19.6 4.2 %all-to-all-start.1 = ((s32[4,1,64]{2,1,0:T(1,128)}), s32[4,1,64]{2,1,0:T(1,128)S(1)}, u32[]{:S(2)}, u32[]{:S(2)}) async-start(s32[4,1,64]{2,1,0:T(1,128)} %broadcast_in_dim.40), calls=%async_computation.1 | async-start | bytes 4096 | tf_op jit(solution)/shard_map/all_to_all | solution.py:9
  23.8 0.1 broadcast_select_fusion
  24.1 3.7 %all-to-all-done.1 = s32[4,1,64]{2,1,0:T(1,128)S(1)} async-done(((s32[4,1,64]{2,1,0:T(1,128)}), s32[4,1,64]{2,1,0:T(1,128)S(1)}, u32[]{:S(2)}, u32[]{:S(2)}) %all-to-all-start.1) | async-done | bytes 1056 | tf_op jit(solution)/shard_map/all_to_all | solution.py:9
  27.8 0.1 broadcast_select_fusion.1
  28.0 0.8 select_reduce_fusion
  28.8 0.7 multiply_add_fusion
  29.5 0.6 broadcast_compare_fusion
  30.1 3.9 %convolution_convert_fusion = bf16[1024,2048]{1,0:T(8,128)(2,1)S(1)} fusion(bf16[512,2048]{1,0:T(8,128)(2,1)} %param.5, s32[512]{0:T(512)S(1)} %multiply_add_fusion, pred[512]{0:T(512)(128)(4,1)S(1)} %get-tuple-element.4), kind=kOutput, calls=%fused_computation | convolution fusion | flops 2150629376 | bytes 6294016 | tf_op jit(solution)/shard_map/dot_general | solution.py:68
  34.0 102.5 %all_to_all.29 = bf16[64,16,2048]{2,1,0:T(8,128)(2,1)S(1)} all-to-all(bf16[64,16,2048]{2,1,0:T(8,128)(2,1)S(1)} %bitcast.42), channel_id=1, replica_groups=mesh['dp'=4,'expert'=64] {'expert'}, dimensions={0} | all-to-all | bytes 8388608 | tf_op jit(solution)/shard_map/all_to_all | solution.py:70
  136.5 1.9 copy-done.1
  138.4 5.2 %fusion.1 = f32[1024,768]{1,0:T(8,128)} fusion(bf16[1024,2048]{1,0:T(8,128)(2,1)S(1)} %bitcast.39, bf16[1,2048,768]{2,1,0:T(8,128)(2,1)S(1)} %copy-done.2), kind=kOutput, calls=%fused_computation.3 | convolution fusion | flops 3221225472 | bytes 10485760 | tf_op jit(solution)/shard_map/dot_general | solution.py:42
  143.6 12.3 %convolution_convert_fusion.1 = bf16[1024,2048]{1,0:T(8,128)(2,1)} fusion(bf16[1,768,2048]{2,1,0:T(8,128)(2,1)S(1)} %copy-done, f32[1024,768]{1,0:T(8,128)} %fusion.1, bf16[1024,2048]{1,0:T(8,128)(2,1)} %bitcast.40, bf16[1,2048,768]{2,1,0:T(8,128)(2,1)} %param.7), kind=kOutput, calls=%fused_computation.1 | convolution fusion | flops 6449266688 | bytes 17825792 | tf_op jit(solution)/shard_map/dot_general | solution.py:44
  155.9 101.7 %all_to_all.30 = bf16[64,16,2048]{2,1,0:T(8,128)(2,1)S(1)} all-to-all(bf16[64,16,2048]{2,1,0:T(8,128)(2,1)} %bitcast.41), channel_id=1, replica_groups=mesh['dp'=4,'expert'=64] {'expert'}, dimensions={0} | all-to-all | bytes 8388608 | tf_op jit(solution)/shard_map/all_to_all | solution.py:73
  257.6 3.8 %convolution_convert_fusion.2 = bf16[512,2048]{1,0:T(8,128)(2,1)} fusion(bf16[1024,2048]{1,0:T(8,128)(2,1)S(1)} %bitcast.38, s32[512]{0:T(512)S(1)} %multiply_add_fusion, pred[512]{0:T(512)(128)(4,1)S(1)} %get-tuple-element.4), kind=kOutput, calls=%fused_computation.8 | convolution fusion | flops 2149580800 | bytes 6294016 | tf_op jit(solution)/shard_map/dot_general | solution.py:81
  (27 shorter events, 0.3 us)
Async XLA Ops:
  0.6 143.0 %copy-start = (bf16[1,768,2048]{2,1,0:T(8,128)(2,1)S(1)}, bf16[1,768,2048]{2,1,0:T(8,128)(2,1)}, u32[]{:S(2)}) copy-start(bf16[1,768,2048]{2,1,0:T(8,128)(2,1)} %param.9) | copy-start | bytes 9437188
  2.2 16.7 %all-to-all-start = ((s32[64,1,64]{2,1,0:T(1,128)}), s32[64,1,64]{2,1,0:T(1,128)S(1)}, u32[]{:S(2)}, u32[]{:S(2)}) async-start(s32[64,1,64]{2,1,0:T(1,128)} %broadcast_in_dim.37), calls=%async_computation | async-start | bytes 65536 | tf_op jit(solution)/shard_map/all_to_all | solution.py:9
  19.6 8.2 %all-to-all-start.1 = ((s32[4,1,64]{2,1,0:T(1,128)}), s32[4,1,64]{2,1,0:T(1,128)S(1)}, u32[]{:S(2)}, u32[]{:S(2)}) async-start(s32[4,1,64]{2,1,0:T(1,128)} %broadcast_in_dim.40), calls=%async_computation.1 | async-start | bytes 4096 | tf_op jit(solution)/shard_map/all_to_all | solution.py:9
  34.0 104.4 %copy-start.2 = (bf16[1,2048,768]{2,1,0:T(8,128)(2,1)S(1)}, bf16[1,2048,768]{2,1,0:T(8,128)(2,1)}, u32[]{:S(2)}) copy-start(bf16[1,2048,768]{2,1,0:T(8,128)(2,1)} %param.8) | copy-start | bytes 9437188
  136.5 1.9 copy-start.1
where the time goes:
time: 266 us; the launch traced here: 261 us
  blocking collectives  204 us (77%)
  matrix products  25.3 us (10%)
  starting transfers between devices  15.2 us (6%)
  waiting for transfers between devices  7.21 us (3%)
  other arithmetic  5.25 us (2%)
  local copies, waits for them, and re-layouts  3.64 us (1%)
    all_to_all x1, blocking collectives, on_device(): lax.all_to_all(outgoing, 'expert', split_axis=0, concat_axis=0, tiled=True)  102 us
    all_to_all x1, blocking collectives, on_device(): lax.all_to_all(expert_ffn(flat, gate_proj, up_proj, down_proj).reshape(so...  102 us
    all_to_all x2, starting transfers between devices, copy_for_each(): return lax.all_to_all(copies, axis, split_axis=0, concat_axis=0, tiled=True)  15.2 us
    dot_general x1, matrix products, expert_ffn(): jnp.dot(hidden, down_proj[0], preferred_element_type=jnp.float32)  12.3 us
    all_to_all x2, waiting for transfers between devices, copy_for_each(): return lax.all_to_all(copies, axis, split_axis=0, concat_axis=0, tiled=True)  7.21 us
  transfers between devices with their start and end apart: 2, of which 2 were waited for; matrix products, arithmetic and copies ran while one was open for 1% of the time, Pallas kernels for 0%

commit v1 on v0

v1 whole, which is shorter than its diff:
```python
import functools

import jax
import jax.numpy as jnp
from jax import lax
from jax.experimental import pallas as pl
from jax.experimental.pallas import tpu as pltpu
from jax.sharding import PartitionSpec as P

NZ, NX, NC = 8, 4, 2
PLANE = NX * NC
LANES = 128


def offset_of(group):
    half, odd = (group + 1) // 2, group % 2
    return (odd * half + (1 - odd) * (NZ - half)) % NZ


def place(me, group, inner, sign):
    z, x, c = me // PLANE, (me // NC) % NX, me % NC
    dz, dx, dc = offset_of(group), inner // NC, inner % NC
    z = (z + sign * dz + NZ) % NZ
    x = (x + sign * dx + NX) % NX
    c = (c + dc) % NC
    return (z * NX + x) * NC + c


def exchange_kernel(
    out_hbm, counts_ref, gate_hbm, up_hbm, down_hbm,
    back_hbm, offset_ref,
    arrived, result, gate_v, up_v, down_v, count_all, total_mine, total_all,
    w_sem, send_sem, recv_sem, bsend_sem, brecv_sem, csend_sem, crecv_sem, tsend_sem, trecv_sem,
):
    me, mine = lax.axis_index("expert"), lax.axis_index("dp")
    n, dps = lax.axis_size("expert"), lax.axis_size("dp")
    groups = n // PLANE
    most, width = arrived.shape[1], arrived.shape[2]

    for k, (src, dst) in enumerate(((gate_hbm, gate_v), (up_hbm, up_v), (down_hbm, down_v))):
        pltpu.make_async_copy(src.at[0], dst, w_sem.at[k]).start()
    own = pltpu.make_async_copy(out_hbm.at[me], arrived.at[0], recv_sem.at[0])

    barrier = pltpu.get_barrier_semaphore()

    def greet(j, carry):
        pl.semaphore_signal(barrier, inc=1, device_id={"expert": (me + j) % n})
        return carry

    lax.fori_loop(1, n, greet, 0)
    for k in range(1, dps):
        pl.semaphore_signal(barrier, inc=1, device_id={"dp": (mine + k) % dps})
    pl.semaphore_wait(barrier, n - 1 + dps - 1)

    def counts_copy(j):
        return pltpu.make_async_remote_copy(
            src_ref=counts_ref, dst_ref=count_all.at[me],
            send_sem=csend_sem, recv_sem=crecv_sem,
            device_id={"expert": (me + j) % n},
        )

    def send_counts(j, carry):
        counts_copy(j).start()
        return carry

    def tokens_copy(group, inner):
        peer = place(me, group, inner, 1)
        slot = group * PLANE + inner
        return pltpu.make_async_remote_copy(
            src_ref=out_hbm.at[peer], dst_ref=arrived.at[slot],
            send_sem=send_sem.at[slot], recv_sem=recv_sem.at[slot],
            device_id={"expert": peer},
        )

    def back_copy(group, inner):
        peer = place(me, group, inner, -1)
        slot = group * PLANE + inner
        return pltpu.make_async_remote_copy(
            src_ref=result.at[slot], dst_ref=back_hbm.at[me],
            send_sem=bsend_sem.at[slot], recv_sem=brecv_sem.at[slot],
            device_id={"expert": peer},
        )

    def back_arrival(group, inner):
        peer = place(me, group, inner, 1)
        slot = group * PLANE + inner
        return pltpu.make_async_remote_copy(
            src_ref=result.at[slot], dst_ref=back_hbm.at[peer],
            send_sem=bsend_sem.at[slot], recv_sem=brecv_sem.at[slot],
            device_id={"expert": peer},
        )

    lax.fori_loop(1, n, send_counts, 0)

    def issue(*members):
        def body(inner, carry):
            for g in members:
                tokens_copy(g, inner).start()
            return carry
        lax.fori_loop(1 if 0 in members else 0, PLANE, body, 0)

    own.start()
    issue(0)
    for g in range(1, groups - 1, 2):
        issue(g, g + 1)
    issue(groups - 1)

    count_all[me] = counts_ref[...]

    others = count_all.at[pl.ds(1, n - 1)]
    for sem in (crecv_sem, csend_sem):
        pltpu.make_async_copy(others, others, sem).wait()
    rows = count_all[...]
    earlier = lax.broadcasted_iota(jnp.int32, rows.shape, 0) < me
    inner_part = jnp.sum(jnp.where(earlier, rows, 0), axis=0)
    total_mine[...] = jnp.sum(rows, axis=0)

    def total_copy(k):
        return pltpu.make_async_remote_copy(
            src_ref=total_mine, dst_ref=total_all.at[mine],
            send_sem=tsend_sem.at[k], recv_sem=trecv_sem.at[k],
            device_id={"dp": (mine + k) % dps},
        )

    for k in range(1, dps):
        total_copy(k).start()
    total_all[mine] = total_mine[...]

    for k, (src, dst) in enumerate(((gate_hbm, gate_v), (up_hbm, up_v), (down_hbm, down_v))):
        pltpu.make_async_copy(src.at[0], dst, w_sem.at[k]).wait()

    def ffn(group, carry):
        def arrive(inner, carry):
            slot = group * PLANE + inner
            pltpu.make_async_copy(out_hbm.at[0], arrived.at[slot], recv_sem.at[slot]).wait()
            return carry

        lax.fori_loop(0, PLANE, arrive, 0)
        rows = arrived[pl.ds(group * PLANE, PLANE)].reshape(PLANE * most, width)
        gate_val = jnp.dot(rows, gate_v[...], preferred_element_type=jnp.float32)
        up_val = jnp.dot(rows, up_v[...], preferred_element_type=jnp.float32)
        hidden = (jax.nn.silu(gate_val) * up_val).astype(jnp.bfloat16)
        mixed = jnp.dot(hidden, down_v[...], preferred_element_type=jnp.float32)
        result[pl.ds(group * PLANE, PLANE)] = mixed.astype(jnp.bfloat16).reshape(PLANE, most, width)

        def give_back(inner, carry):
            slot = group * PLANE + inner

            @pl.when(slot > 0)
            def _():
                back_copy(group, inner).start()

            @pl.when(slot == 0)
            def _():
                pltpu.make_async_copy(result.at[0], back_hbm.at[me], brecv_sem.at[0]).start()
            return carry

        lax.fori_loop(0, PLANE, give_back, 0)
        return carry

    lax.fori_loop(0, groups, ffn, 0)

    for k in range(1, dps):
        total_copy(k).wait()
    totals = total_all[...]
    before = lax.broadcasted_iota(jnp.int32, totals.shape, 0) < mine
    offset_ref[...] = inner_part + jnp.sum(jnp.where(before, totals, 0), axis=0)

    pltpu.make_async_copy(result.at[0], back_hbm.at[me], brecv_sem.at[0]).wait()

    def finish(slot, carry):
        group, inner = slot // PLANE, slot % PLANE
        tokens_copy(group, inner).wait_send()
        back_copy(group, inner).wait_send()
        back_arrival(group, inner).wait_recv()
        return carry

    lax.fori_loop(1, n, finish, 0)


def exchange(outgoing, counts, gate_proj, up_proj, down_proj):
    n, most, width = outgoing.shape
    dps = lax.axis_size("dp")
    hidden = gate_proj.shape[2]
    vmem, hbm = pl.BlockSpec(memory_space=pltpu.VMEM), pl.BlockSpec(memory_space=pl.ANY)
    return pl.pallas_call(
        exchange_kernel,
        out_shape=(
            jax.ShapeDtypeStruct(outgoing.shape, jnp.bfloat16),
            jax.ShapeDtypeStruct((1, LANES), jnp.int32),
        ),
        in_specs=[hbm, vmem, hbm, hbm, hbm],
        out_specs=(hbm, vmem),
        scratch_shapes=[
            pltpu.VMEM((n, most, width), jnp.bfloat16),
            pltpu.VMEM((n, most, width), jnp.bfloat16),
            pltpu.VMEM((width, hidden), jnp.bfloat16),
            pltpu.VMEM((width, hidden), jnp.bfloat16),
            pltpu.VMEM((hidden, width), jnp.bfloat16),
            pltpu.VMEM((n, 1, LANES), jnp.int32),
            pltpu.VMEM((1, LANES), jnp.int32),
            pltpu.VMEM((dps, 1, LANES), jnp.int32),
            pltpu.SemaphoreType.DMA((3,)),
            pltpu.SemaphoreType.DMA((n,)),
            pltpu.SemaphoreType.DMA((n,)),
            pltpu.SemaphoreType.DMA((n,)),
            pltpu.SemaphoreType.DMA((n,)),
            pltpu.SemaphoreType.DMA,
            pltpu.SemaphoreType.DMA,
            pltpu.SemaphoreType.DMA((dps,)),
            pltpu.SemaphoreType.DMA((dps,)),
        ],
        compiler_params=pltpu.CompilerParams(
            collective_id=0, has_side_effects=True, vmem_limit_bytes=48 * 1024 * 1024
        ),
        cost_estimate=pl.CostEstimate(
            flops=6 * n * most * width * hidden,
            bytes_accessed=3 * width * hidden * 2 + 4 * n * most * width,
            transcendentals=n * most * hidden,
        ),
    )(outgoing, counts, gate_proj, up_proj, down_proj)


def on_device(tokens, expert_ids, gate_proj, up_proj, down_proj):
    tok_rows, width = tokens.shape
    experts_all = lax.axis_size("expert")
    most = 2 * tok_rows // experts_all
    capacity = tok_rows * lax.axis_size("dp")
    choices = expert_ids[:, 0]
    hot = choices[:, None] == jnp.arange(LANES, dtype=jnp.int32)[None, :]
    onehot = hot.astype(jnp.int32)
    counts = jnp.sum(onehot, axis=0)[None, :]
    earlier = jnp.arange(tok_rows)[:, None] > jnp.arange(tok_rows)[None, :]
    before = jnp.dot(
        earlier.astype(jnp.bfloat16), hot.astype(jnp.bfloat16), preferred_element_type=jnp.float32
    )
    local_rank = jnp.sum(jnp.where(hot, before, 0.0), axis=1).astype(jnp.int32)
    position = choices * most + local_rank
    targets = jnp.arange(experts_all * most, dtype=jnp.int32)
    dispatch = (targets[:, None] == position[None, :]).astype(jnp.bfloat16)
    outgoing = jnp.dot(dispatch, tokens, preferred_element_type=jnp.float32).astype(jnp.bfloat16)
    outgoing = outgoing.reshape(experts_all, most, width)
    returned, offset = exchange(outgoing, counts, gate_proj, up_proj, down_proj)
    flat_back = returned.reshape(experts_all * most, width)
    global_slot = (jnp.sum(onehot * offset, axis=1) + local_rank).astype(jnp.int32)
    is_kept = global_slot < capacity
    combine = ((position[:, None] == targets[None, :]) & is_kept[:, None]).astype(jnp.bfloat16)
    mixed = jnp.dot(combine, flat_back, preferred_element_type=jnp.float32)
    return (mixed.astype(jnp.bfloat16), global_slot)


def solution(mesh):
    in_specs = (
        P(("dp", "expert"), None),
        P(("dp", "expert"), None),
        P("expert", None, None),
        P("expert", None, None),
        P("expert", None, None),
    )
    out_specs = (P(("dp", "expert"), None), P(("dp", "expert")))
    return jax.shard_map(
        on_device, mesh=mesh, in_specs=in_specs, out_specs=out_specs, check_vma=False
    )
```

time: 266 us -> 224 us (0.84)
  Pallas kernels: 0 us -> 207 us
  blocking collectives: 204 us -> 0 us
  starting transfers between devices: 15.2 us -> 0 us
  matrix products: 25.3 us -> 11.3 us
  waiting for transfers between devices: 7.21 us -> 0 us
  other arithmetic: 5.25 us -> 1.5 us
  local copies, waits for them, and re-layouts: 3.64 us -> 0.02 us
    pallas_call x0 -> x1, Pallas kernels: none -> 207 us  [exchange(): pl.pallas_call(exchange_kernel, out_shape=(jax.ShapeDtypeStruct(outgoing....]
    all_to_all x2 -> x0, blocking collectives: 204 us -> none  [the longest x1 102 us: on_device(): lax.all_to_all(outgoing, 'expert', split_axis=0, concat_axis=0, tiled=True)]
    all_to_all x2 -> x0, starting transfers between devices: 15.2 us -> none  [copy_for_each(): return lax.all_to_all(copies, axis, split_axis=0, concat_axis=0, tiled=True)]
    dot_general x3 -> x2, matrix products: 21.3 us -> 7.08 us  [the longest x1 5.93 us: on_device(): mixed = jnp.dot(combine, flat_back, preferred_element_type=jnp.float32)]
    all_to_all x2 -> x0, waiting for transfers between devices: 7.21 us -> none  [copy_for_each(): return lax.all_to_all(copies, axis, split_axis=0, concat_axis=0, tiled=True)]
  transfers between devices with their start and end apart: 2 -> 0, of which waited for: 2 -> 0; matrix products, arithmetic and copies ran while one was open for 1% -> 0% of each run, Pallas kernels for 0% -> 0%
where the time goes in v1:
time: 224 us; the launch traced here: 220 us
  Pallas kernels  207 us (92%)
  matrix products  11.3 us (5%)
    pallas_call x1, Pallas kernels, exchange(): pl.pallas_call(exchange_kernel, out_shape=(jax.ShapeDtypeStruct(outgoing....  207 us
    dot_general x1, matrix products, on_device(): mixed = jnp.dot(combine, flat_back, preferred_element_type=jnp.float32)  5.93 us

profile of v1, /device:TPU:99, one launch (start us, length us, event | category | flops | bytes accessed | tf_op | source)
XLA Modules:
  0.0 220.2 jit_solution(15849024461359828172)
XLA Ops:
  0.6 0.0 copy-start
  0.6 1.2 fusion.2
  1.8 0.7 multiply_add_fusion
  2.5 0.0 copy-done
  2.5 0.0 copy-start.2
  2.5 0.0 copy-start.1
  2.5 4.3 %convolution_convert_fusion = bf16[1024,2048]{1,0:T(8,128)(2,1)} fusion(bf16[512,2048]{1,0:T(8,128)(2,1)S(1)} %copy-done, s32[512]{0:T(512)S(1)} %multiply_add_fusion), kind=kOutput, calls=%fused_computation | convolution fusion | flops 2150105088 | bytes 6293504 | tf_op jit(solution)/shard_map/dot_general | solution.py:241
  6.8 0.0 copy-done.2
  6.8 0.1 convert_reduce_fusion
  6.9 0.0 copy-done.1
  6.9 206.7 %shard_map.68 = (bf16[64,16,2048]{2,1,0:T(8,128)(2,1)}, s32[1,128]{1,0:T(1,128)S(1)}) custom-call(bf16[64,16,2048]{2,1,0:T(8,128)(2,1)} %bitcast.18, s32[1,128]{1,0:T(1,128)S(1)} %bitcast.10, bf16[1,2048,768]{2,1,0:T(8,128)(2,1)S(1)} %copy-done.1, bf16[1,2048,768]{2,1,0:T(8,128)(2,1)} %up_hbm.1, bf16[1,768,2048]{2,1,0:T(8,128)(2,1)} %down_hbm.1), custom_call_target="tpu_custom_call" | custom-call | flops 9663676416 | bytes 17825792 | tf_op jit(solution)/shard_map/pallas_call | solution.py:186
  213.6 0.1 select_reduce_fusion
  213.7 0.6 broadcast_compare_fusion
  214.3 5.9 %convolution_convert_fusion.1 = bf16[512,2048]{1,0:T(8,128)(2,1)} fusion(bf16[1024,2048]{1,0:T(8,128)(2,1)} %bitcast.17, s32[512]{0:T(512)S(1)} %bitcast.16, pred[512]{0:T(512)(128)(4,1)S(1)} %get-tuple-element.6), kind=kOutput, calls=%fused_computation.1 | convolution fusion | flops 2149580800 | bytes 6294016 | tf_op jit(solution)/shard_map/dot_general | solution.py:248
  (2 shorter events, 0.0 us)
Async XLA Ops:
  0.6 1.9 copy-start
  2.5 4.3 %copy-start.2 = (s32[512,1]{0,1:T(1,128)S(1)}, s32[512,1]{0,1:T(1,128)}, u32[]{:S(2)}) copy-start(s32[512,1]{0,1:T(1,128)} %param.6) | copy-start | bytes 6148
  2.5 4.4 %copy-start.1 = (bf16[1,2048,768]{2,1,0:T(8,128)(2,1)S(1)}, bf16[1,2048,768]{2,1,0:T(8,128)(2,1)}, u32[]{:S(2)}) copy-start(bf16[1,2048,768]{2,1,0:T(8,128)(2,1)} %gate_hbm.1) | copy-start | bytes 9437188

commit v2 on v0

v2 whole, which is shorter than its diff:
```python
import functools

import jax
import jax.numpy as jnp
from jax import lax
from jax.experimental import pallas as pl
from jax.experimental.pallas import tpu as pltpu
from jax.sharding import PartitionSpec as P

NX, NC = 4, 2
PLANE = NX * NC
LANES = 128
LEVELS = (80, 96, 112)


def mate_of(p, inner, sign):
    x, c = p // NC, p % NC
    x = (x + sign * (inner // NC) + NX) % NX
    c = (c + inner % NC) % NC
    return x * NC + c


def offset_of(group, planes):
    half, odd = (group + 1) // 2, group % 2
    return (odd * half + (1 - odd) * (planes - half)) % planes


def greet(axis, peers, size):
    barrier = pltpu.get_barrier_semaphore()
    for peer in peers:
        pl.semaphore_signal(barrier, inc=1, device_id={axis: peer})


def survey_kernel(
    tokens, places, row, outgoing, meta, offset, largest,
    near, far, mine_sum, sums, asend, arecv, bsend, brecv, csend, crecv,
):
    me, dp = lax.axis_index("expert"), lax.axis_index("dp")
    n, dps = lax.axis_size("expert"), lax.axis_size("dp")
    planes = n // PLANE
    z, p = me // PLANE, me % PLANE
    barrier = pltpu.get_barrier_semaphore()
    greet("expert", [z * PLANE + mate_of(p, i, 1) for i in range(1, PLANE)], n)
    greet("expert", [(z + k) % planes * PLANE + p for k in range(1, planes)], n)
    greet("dp", [(dp + k) % dps for k in range(1, dps)], dps)
    pl.semaphore_wait(barrier, PLANE - 1 + planes - 1 + dps - 1)

    def near_copy(i):
        return pltpu.make_async_remote_copy(
            src_ref=row, dst_ref=near.at[p], send_sem=asend.at[i], recv_sem=arecv.at[i],
            device_id={"expert": z * PLANE + mate_of(p, i, 1)},
        )

    def far_copy(k):
        return pltpu.make_async_remote_copy(
            src_ref=near, dst_ref=far.at[z], send_sem=bsend.at[k], recv_sem=brecv.at[k],
            device_id={"expert": (z + k) % planes * PLANE + p},
        )

    def sum_copy(k):
        return pltpu.make_async_remote_copy(
            src_ref=mine_sum, dst_ref=sums.at[dp], send_sem=csend.at[k], recv_sem=crecv.at[k],
            device_id={"dp": (dp + k) % dps},
        )

    def pack(k, carry):
        at = places[...]
        targets = lax.broadcasted_iota(jnp.int32, (LANES, at.shape[1]), 0) + k * LANES
        dispatch = (targets == at[0:1]).astype(jnp.float32).astype(jnp.bfloat16)
        outgoing[k] = jnp.dot(
            dispatch, tokens[...], preferred_element_type=jnp.float32
        ).astype(jnp.bfloat16)
        marks = jnp.broadcast_to(at[1:2], (8, at.shape[1])).astype(jnp.float32).astype(jnp.bfloat16)
        named = lax.dot_general(
            marks, dispatch, (((1,), (1,)), ((), ())), preferred_element_type=jnp.float32
        )
        meta[k] = named[0:1].astype(jnp.int32) - 1
        return carry

    for i in range(1, PLANE):
        near_copy(i).start()
    near[p] = row[...]
    lax.fori_loop(0, 3, pack, 0)
    for i in range(1, PLANE):
        near_copy(i).wait()
    for k in range(1, planes):
        far_copy(k).start()
    far[z] = near[...]
    lax.fori_loop(3, 6, pack, 0)
    for k in range(1, planes):
        far_copy(k).wait()
    rows = far[...].reshape(n, 1, LANES)
    earlier = lax.broadcasted_iota(jnp.int32, rows.shape, 0) < me
    inner_part = jnp.sum(jnp.where(earlier, rows, 0), axis=0)
    experts_lane = lax.broadcasted_iota(jnp.int32, (1, LANES), 1) < n
    mine_sum[...] = jnp.where(experts_lane, jnp.sum(rows, axis=0), jnp.max(rows, axis=0))
    for k in range(1, dps):
        sum_copy(k).start()
    sums[dp] = mine_sum[...]
    lax.fori_loop(6, planes, pack, 0)
    for k in range(1, dps):
        sum_copy(k).wait()
    totals = sums[...]
    before = lax.broadcasted_iota(jnp.int32, totals.shape, 0) < dp
    offset[...] = inner_part + jnp.sum(jnp.where(before, totals, 0), axis=0)
    largest[...] = jnp.where(experts_lane, 0, jnp.max(totals, axis=0))


def survey(tokens, places, row):
    n, dps = lax.axis_size("expert"), lax.axis_size("dp")
    planes, width = n // PLANE, tokens.shape[1]
    vmem = pl.BlockSpec(memory_space=pltpu.VMEM)
    return pl.pallas_call(
        survey_kernel,
        out_shape=(
            jax.ShapeDtypeStruct((planes, LANES, width), jnp.bfloat16),
            jax.ShapeDtypeStruct((planes, 1, LANES), jnp.int32),
            jax.ShapeDtypeStruct((1, LANES), jnp.int32),
            jax.ShapeDtypeStruct((1, LANES), jnp.int32),
        ),
        in_specs=[vmem] * 3,
        out_specs=(vmem,) * 4,
        scratch_shapes=[
            pltpu.VMEM((PLANE, 1, LANES), jnp.int32),
            pltpu.VMEM((planes, PLANE, 1, LANES), jnp.int32),
            pltpu.VMEM((1, LANES), jnp.int32),
            pltpu.VMEM((dps, 1, LANES), jnp.int32),
            pltpu.SemaphoreType.DMA((PLANE,)),
            pltpu.SemaphoreType.DMA((PLANE,)),
            pltpu.SemaphoreType.DMA((planes,)),
            pltpu.SemaphoreType.DMA((planes,)),
            pltpu.SemaphoreType.DMA((dps,)),
            pltpu.SemaphoreType.DMA((dps,)),
        ],
        compiler_params=pltpu.CompilerParams(
            collective_id=0, has_side_effects=True, vmem_limit_bytes=24 * 1024 * 1024
        ),
    )(tokens, places, row)


def exchange_kernel(
    cap, outgoing, meta, gate_hbm, up_hbm, down_hbm, back_hbm,
    relay, relay_meta, spread, arrived, result, gathered, packed, gate_v, up_v, down_v,
    w_sem, zsend, zrecv, msend, mrecv, xsend, xrecv, rsend, rrecv, bsend, brecv,
):
    me = lax.axis_index("expert")
    n = lax.axis_size("expert")
    planes, most = n // PLANE, arrived.shape[2]
    width = arrived.shape[3]
    z, p = me // PLANE, me % PLANE
    weights = ((gate_hbm, gate_v), (up_hbm, up_v), (down_hbm, down_v))

    def weight_copy(k):
        src, dst = weights[k]
        return pltpu.make_async_copy(src.at[0], dst, w_sem.at[k])

    for k in range(3):
        weight_copy(k).start()
    barrier = pltpu.get_barrier_semaphore()
    greet("expert", [z * PLANE + mate_of(p, i, 1) for i in range(1, PLANE)], n)
    greet("expert", [(z + k) % planes * PLANE + p for k in range(1, planes)], n)
    pl.semaphore_wait(barrier, PLANE - 1 + planes - 1)

    def plane_at(group, sign):
        return (z + sign * offset_of(group, planes) + planes) % planes

    def meta_copy(group):
        to = plane_at(group, 1)
        return pltpu.make_async_remote_copy(
            src_ref=meta.at[to], dst_ref=relay_meta.at[group],
            send_sem=msend.at[group], recv_sem=mrecv.at[group],
            device_id={"expert": to * PLANE + p},
        )

    def bucket_copy(group):
        to = plane_at(group, 1)
        return pltpu.make_async_remote_copy(
            src_ref=outgoing.at[to, pl.ds(0, cap)], dst_ref=relay.at[group],
            send_sem=zsend.at[group], recv_sem=zrecv.at[group],
            device_id={"expert": to * PLANE + p},
        )

    def spread_copy(group, inner):
        mate = mate_of(p, inner, 1)
        at = group * PLANE + inner
        return pltpu.make_async_remote_copy(
            src_ref=spread.at[group, mate], dst_ref=arrived.at[group, p],
            send_sem=xsend.at[at], recv_sem=xrecv.at[at],
            device_id={"expert": z * PLANE + mate},
        )

    def gather_copy(group, inner):
        mate = mate_of(p, inner, -1)
        at = group * PLANE + inner
        return pltpu.make_async_remote_copy(
            src_ref=result.at[group, mate], dst_ref=gathered.at[group, p],
            send_sem=rsend.at[at], recv_sem=rrecv.at[at],
            device_id={"expert": z * PLANE + mate},
        )

    def back_copy(group):
        return pltpu.make_async_remote_copy(
            src_ref=packed.at[group], dst_ref=back_hbm.at[z],
            send_sem=bsend.at[group], recv_sem=brecv.at[group],
            device_id={"expert": plane_at(group, -1) * PLANE + p},
        )

    own_back = pltpu.make_async_copy(packed.at[0], back_hbm.at[z], brecv.at[0])

    def issue(group, carry):
        meta_copy(group).start()
        bucket_copy(group).start()
        return carry

    lax.fori_loop(1, planes, issue, 0)
    relay_meta[0] = meta[z]
    relay[0] = outgoing[z, 0:cap]
    for k in range(3):
        weight_copy(k).wait()

    def routes(group):
        targets = lax.broadcasted_iota(jnp.int32, (PLANE * most, cap), 0)
        named = relay_meta[group][:, 0:cap]
        return (targets == named).astype(jnp.float32).astype(jnp.bfloat16)

    def scatter(group):
        @pl.when(group > 0)
        def _():
            meta_copy(group).wait_recv()
            bucket_copy(group).wait_recv()

        rows = jnp.dot(routes(group), relay[group], preferred_element_type=jnp.float32)
        spread[group] = rows.astype(jnp.bfloat16).reshape(PLANE, most, width)

        def send(inner, carry):
            spread_copy(group, inner).start()
            return carry

        lax.fori_loop(1, PLANE, send, 0)
        arrived[group, p] = spread[group, p]

    def ffn(group):
        def arrive(inner, carry):
            spread_copy(group, inner).wait_recv()
            return carry

        lax.fori_loop(1, PLANE, arrive, 0)
        rows = arrived[group].reshape(PLANE * most, width)
        gate_val = jnp.dot(rows, gate_v[...], preferred_element_type=jnp.float32)
        up_val = jnp.dot(rows, up_v[...], preferred_element_type=jnp.float32)
        hidden = (jax.nn.silu(gate_val) * up_val).astype(jnp.bfloat16)
        mixed = jnp.dot(hidden, down_v[...], preferred_element_type=jnp.float32)
        result[group] = mixed.astype(jnp.bfloat16).reshape(PLANE, most, width)

        def send(inner, carry):
            gather_copy(group, inner).start()
            return carry

        lax.fori_loop(1, PLANE, send, 0)
        gathered[group, p] = result[group, p]

    def give_back(group):
        def arrive(inner, carry):
            gather_copy(group, inner).wait_recv()
            return carry

        lax.fori_loop(1, PLANE, arrive, 0)
        rows = gathered[group].reshape(PLANE * most, width)
        packed[group] = lax.dot_general(
            routes(group), rows, (((0,), (0,)), ((), ())), preferred_element_type=jnp.float32
        ).astype(jnp.bfloat16)

        @pl.when(group > 0)
        def _():
            back_copy(group).start()

        @pl.when(group == 0)
        def _():
            own_back.start()

    def step(i, carry):
        @pl.when(i < planes)
        def _():
            scatter(i)

        @pl.when((i >= 1) & (i <= planes))
        def _():
            ffn(i - 1)

        @pl.when(i >= 2)
        def _():
            give_back(i - 2)

        return carry

    lax.fori_loop(0, planes + 2, step, 0)

    def finish(group, carry):
        meta_copy(group).wait_send()
        bucket_copy(group).wait_send()
        back_copy(group).wait()
        return carry

    def finish_near(at, carry):
        group, inner = at // (PLANE - 1), at % (PLANE - 1) + 1
        spread_copy(group, inner).wait_send()
        gather_copy(group, inner).wait_send()
        return carry

    own_back.wait()
    lax.fori_loop(0, planes * (PLANE - 1), finish_near, 0)
    lax.fori_loop(1, planes, finish, 0)


def exchange(level, cap, most, outgoing, meta, gate_proj, up_proj, down_proj):
    planes, _, width = outgoing.shape
    hidden = gate_proj.shape[2]
    vmem, hbm = pl.BlockSpec(memory_space=pltpu.VMEM), pl.BlockSpec(memory_space=pl.ANY)
    blocks = (planes, PLANE, most, width)
    near = (planes * PLANE,)
    return pl.pallas_call(
        functools.partial(exchange_kernel, cap),
        out_shape=jax.ShapeDtypeStruct((planes, cap, width), jnp.bfloat16),
        in_specs=[vmem, vmem, hbm, hbm, hbm],
        out_specs=hbm,
        scratch_shapes=[
            pltpu.VMEM((planes, cap, width), jnp.bfloat16),
            pltpu.VMEM((planes, 1, LANES), jnp.int32),
            pltpu.VMEM(blocks, jnp.bfloat16),
            pltpu.VMEM(blocks, jnp.bfloat16),
            pltpu.VMEM(blocks, jnp.bfloat16),
            pltpu.VMEM(blocks, jnp.bfloat16),
            pltpu.VMEM((planes, cap, width), jnp.bfloat16),
            pltpu.VMEM((width, hidden), jnp.bfloat16),
            pltpu.VMEM((width, hidden), jnp.bfloat16),
            pltpu.VMEM((hidden, width), jnp.bfloat16),
            pltpu.SemaphoreType.DMA((3,)),
            pltpu.SemaphoreType.DMA((planes,)),
            pltpu.SemaphoreType.DMA((planes,)),
            pltpu.SemaphoreType.DMA((planes,)),
            pltpu.SemaphoreType.DMA((planes,)),
            pltpu.SemaphoreType.DMA(near),
            pltpu.SemaphoreType.DMA(near),
            pltpu.SemaphoreType.DMA(near),
            pltpu.SemaphoreType.DMA(near),
            pltpu.SemaphoreType.DMA((planes,)),
            pltpu.SemaphoreType.DMA((planes,)),
        ],
        compiler_params=pltpu.CompilerParams(
            collective_id=1 + level, has_side_effects=True, vmem_limit_bytes=56 * 1024 * 1024
        ),
    )(outgoing, meta, gate_proj, up_proj, down_proj)


def on_device(tokens, expert_ids, gate_proj, up_proj, down_proj):
    tok_rows, width = tokens.shape
    experts_all = lax.axis_size("expert")
    planes = experts_all // PLANE
    most = 2 * tok_rows // experts_all
    capacity = tok_rows * lax.axis_size("dp")
    choices = expert_ids[:, 0]
    plane = choices // PLANE
    lanes = jnp.arange(LANES, dtype=jnp.int32)[None, :]
    by_expert = lanes == choices[:, None]
    by_plane = lanes == experts_all + plane[:, None]
    hot = (by_expert | by_plane).astype(jnp.bfloat16)
    row = jnp.sum(hot.astype(jnp.int32), axis=0)[None, :]
    earlier = jnp.arange(tok_rows)[:, None] > jnp.arange(tok_rows)[None, :]
    before = jnp.dot(earlier.astype(jnp.bfloat16), hot, preferred_element_type=jnp.float32)
    local_rank = jnp.sum(jnp.where(by_expert, before, 0.0), axis=1).astype(jnp.int32)
    plane_rank = jnp.sum(jnp.where(by_plane, before, 0.0), axis=1).astype(jnp.int32)
    places = jnp.stack(
        [plane * LANES + plane_rank, choices % PLANE * most + local_rank + 1]
    )
    outgoing, meta, offset, largest = survey(tokens, places, row)
    global_slot = jnp.sum(jnp.where(by_expert, offset, 0), axis=1) + local_rank
    is_kept = global_slot < capacity

    def at_capacity(level, cap):
        def run(outgoing, meta, plane, plane_rank, is_kept, gate_proj, up_proj, down_proj):
            back = exchange(level, cap, most, outgoing, meta, gate_proj, up_proj, down_proj)
            position = plane * cap + plane_rank
            targets = jnp.arange(planes * cap, dtype=jnp.int32)
            combine = (position[:, None] == targets[None, :]) & is_kept[:, None]
            mixed = jnp.dot(
                combine.astype(jnp.bfloat16),
                back.reshape(planes * cap, width),
                preferred_element_type=jnp.float32,
            )
            return mixed.astype(jnp.bfloat16)

        return run

    caps = LEVELS + (PLANE * most,)
    need = jnp.max(largest)
    level = sum((need > cap).astype(jnp.int32) for cap in LEVELS)
    mixed = lax.switch(
        level,
        [at_capacity(k, cap) for k, cap in enumerate(caps)],
        outgoing, meta, plane, plane_rank, is_kept, gate_proj, up_proj, down_proj,
    )
    return (mixed, global_slot)


def solution(mesh):
    in_specs = (
        P(("dp", "expert"), None),
        P(("dp", "expert"), None),
        P("expert", None, None),
        P("expert", None, None),
        P("expert", None, None),
    )
    out_specs = (P(("dp", "expert"), None), P(("dp", "expert")))
    return jax.shard_map(
        on_device, mesh=mesh, in_specs=in_specs, out_specs=out_specs, check_vma=False
    )
```

time: 266 us -> 185 us (0.70)
  the two profiles are of different devices: /device:TPU:99 before, /device:TPU:1 now
where the time goes in v2:
time: 185 us
  Pallas kernels  170 us (92%)
  matrix products  4.82 us (3%)
  other arithmetic  4.33 us (2%)
  local copies, waits for them, and re-layouts  2.91 us (2%)
  between operations  2.66 us (1%)
    pallas_call x1, Pallas kernels, exchange(): pl.pallas_call(functools.partial(exchange_kernel, cap), out_shape=jax.Sha...  148 us
    pallas_call x1, Pallas kernels, survey(): pl.pallas_call(survey_kernel, out_shape=(jax.ShapeDtypeStruct((planes, LA...  21.8 us
    dot_general x1, matrix products, run(): jnp.dot(combine.astype(jnp.bfloat16), back.reshape(planes * cap, width),...  3.76 us

profile of v2, /device:TPU:1, one launch (start us, length us, event | category | flops | bytes accessed | tf_op | source)
XLA Modules:
  0.0 185.1 jit_solution(4772627180891679407)
XLA Ops:
  0.6 0.0 copy-start.1
  0.6 0.8 add_select_fusion
  1.4 0.7 fusion.29
  2.1 0.8 convert_reduce_fusion
  2.9 1.1 select_reduce_fusion.2
  4.0 0.7 multiply_add_fusion.4
  4.7 0.0 copy-start
  4.7 1.6 copy-done
  6.3 21.8 %shard_map.68 = (bf16[8,128,2048]{2,1,0:T(8,128)(2,1)}, s32[8,1,128]{2,1,0:T(1,128)S(1)}, s32[1,128]{1,0:T(1,128)S(1)}, s32[1,128]{1,0:T(1,128)S(1)}) custom-call(bf16[512,2048]{1,0:T(8,128)(2,1)S(1)} %copy-done, s32[2,512]{1,0:T(2,128)S(1)} %pad_add_fusion.places, s32[1,128]{1,0:T(1,128)S(1)} %bitcast.31), custom_call_target="tpu_custom_call" | custom-call | tf_op jit(solution)/shard_map/pallas_call | solution.py:113
  28.2 0.6 reduce_max.9
  30.7 0.0 copy-done.1
  30.8 0.1 select_reduce_fusion
  30.9 0.6 broadcast_compare_fusion
  31.5 152.3 %conditional.2 = (bf16[512,2048]{1,0:T(8,128)(2,1)S(1)}) conditional(s32[]{:T(128)} %clamp.3, (s32[512]{0:T(512)S(1)}, s32[512]{0:T(512)S(1)}, pred[512]{0:T(512)(128)(4,1)S(1)}, bf16[8,128,2048]{2,1,0:T(8,128)(2,1)}, s32[8,1,128]{2,1,0:T(1,128)S(1)}, /*index=5*/bf16[1,2048,768]{2,1,0:T(8,128)(2,1)}, ...), branch_computations={%region_5.6_spmd, %region_6.7_spmd, %region_7.8_spmd, %region_8.9_... | conditional | flops 2148533248 | bytes 6300168
  31.5 148.3 %branch_1_fun.1 = bf16[8,96,2048]{2,1,0:T(8,128)(2,1)} custom-call(bf16[8,128,2048]{2,1,0:T(8,128)(2,1)} %get-tuple-element.82.outgoing, s32[8,1,128]{2,1,0:T(1,128)S(1)} %get-tuple-element.83.meta, bf16[1,2048,768]{2,1,0:T(8,128)(2,1)} %get-tuple-element.84.gate_hbm, bf16[1,2048,768]{2,1,0:T(8,128)(2,1)} %get-tuple-element.85.up_hbm, ...), custom_call_target="tpu_custom_call" | custom-call | tf_op jit(solution)/shard_map/cond/branch_1_fun/pallas_call | solution.py:321
  179.8 3.8 %fusion.6 = bf16[512,2048]{1,0:T(8,128)(2,1)S(1)} fusion(bf16[768,2048]{1,0:T(8,128)(2,1)} %bitcast.35, s32[512]{0:T(512)S(1)} %multiply_add_fusion.1, pred[512]{0:T(512)(128)(4,1)S(1)} %get-tuple-element.81), kind=kOutput, calls=%fused_computation.8 | convolution fusion | flops 1611399168 | bytes 5245440 | tf_op jit(solution)/shard_map/cond/branch_1_fun/dot_general | solution.py:385
  183.8 0.0 copy-start.2
  183.8 1.3 copy-done.2
  (4 shorter events, 0.0 us)
Async XLA Ops:
  0.6 30.1 %copy-start.1 = (s32[512,1]{0,1:T(1,128)S(1)}, s32[512,1]{0,1:T(1,128)}, u32[]{:S(2)}) copy-start(s32[512,1]{0,1:T(1,128)} %param.10) | copy-start | bytes 6148
  4.7 1.6 copy-start
  183.8 1.3 copy-start.2

commit v3 on v2

v3 whole, which is shorter than its diff:
```python
import functools

import jax
import jax.numpy as jnp
from jax import lax
from jax.experimental import pallas as pl
from jax.experimental.pallas import tpu as pltpu
from jax.sharding import PartitionSpec as P

NX, NC = 4, 2
PLANE = NX * NC
LANES = 128
LEVELS = (64, 72, 80, 96)
LAG = 3


def mate_of(p, inner, sign):
    x, c = p // NC, p % NC
    x = (x + sign * (inner // NC) + NX) % NX
    c = (c + inner % NC) % NC
    return x * NC + c


def offset_of(group, planes):
    back = planes - 1 - group
    half, odd = (back + 1) // 2, back % 2
    return (odd * half + (1 - odd) * (planes - half)) % planes


def greet(axis, peers):
    barrier = pltpu.get_barrier_semaphore()
    for peer in peers:
        pl.semaphore_signal(barrier, inc=1, device_id={axis: peer})


def iota(shape, axis):
    return lax.broadcasted_iota(jnp.int32, shape, axis)


def ones_where(mask):
    return mask.astype(jnp.float32).astype(jnp.bfloat16)


def dot(a, b, dims=((1,), (0,))):
    return lax.dot_general(a, b, (dims, ((), ())), preferred_element_type=jnp.float32)


def to_bf16(x):
    return x.astype(jnp.float32).astype(jnp.bfloat16)


def survey_kernel(
    capacity, most, ids_ref, place_ref, slot_ref, merge_ref, meta_ref, level_ref,
    row, near, far, everyone, asend, arecv, bsend, brecv, csend, crecv,
):
    me, dp = lax.axis_index("expert"), lax.axis_index("dp")
    n, dps = lax.axis_size("expert"), lax.axis_size("dp")
    planes, share = n // PLANE, LANES // dps
    z, p = me // PLANE, me % PLANE
    tok_rows = ids_ref.shape[1]
    greet("expert", [z * PLANE + mate_of(p, i, 1) for i in range(1, PLANE)])
    greet("expert", [(z + k) % planes * PLANE + p for k in range(1, planes)])
    greet("dp", [(dp + k) % dps for k in range(1, dps)])

    def near_copy(i):
        return pltpu.make_async_remote_copy(
            src_ref=row, dst_ref=near.at[p], send_sem=asend.at[i], recv_sem=arecv.at[i],
            device_id={"expert": z * PLANE + mate_of(p, i, 1)},
        )

    def far_copy(k):
        return pltpu.make_async_remote_copy(
            src_ref=near, dst_ref=far.at[z], send_sem=bsend.at[k], recv_sem=brecv.at[k],
            device_id={"expert": (z + k) % planes * PLANE + p},
        )

    def dp_copy(k):
        return pltpu.make_async_remote_copy(
            src_ref=far, dst_ref=everyone.at[dp], send_sem=csend.at[k], recv_sem=crecv.at[k],
            device_id={"dp": (dp + k) % dps},
        )

    ids = ids_ref[...]
    named = iota((LANES, tok_rows), 0) == ids
    hot = ones_where(named)
    counts = dot(jnp.ones((8, tok_rows), jnp.bfloat16), hot, ((1,), (1,)))
    row[...] = counts[0:1].astype(jnp.int32)
    pl.semaphore_wait(pltpu.get_barrier_semaphore(), PLANE - 1 + planes - 1 + dps - 1)

    for i in range(1, PLANE):
        near_copy(i).start()
    near[p] = row[...]
    ahead = ones_where(iota((tok_rows, tok_rows), 0) < iota((tok_rows, tok_rows), 1))
    before = dot(hot, ahead)
    rank = jnp.sum(jnp.where(named, before, 0.0), axis=0, keepdims=True).astype(jnp.int32)
    for i in range(1, PLANE):
        near_copy(i).wait()
    for k in range(1, planes):
        far_copy(k).start()
    far[z] = near[...]
    for k in range(1, planes):
        far_copy(k).wait()
    for k in range(1, dps):
        dp_copy(k).start()
    everyone[dp] = far[...]
    for k in range(1, dps):
        dp_copy(k).wait()

    total = dps * n
    table = everyone[...].reshape(total, LANES)
    lower = ones_where(iota((total, total), 1) < iota((total, total), 0))
    ahead_of = dot(lower, to_bf16(table)).astype(jnp.int32)
    kept = jnp.clip(capacity - ahead_of, 0, table)
    of_dps = sum(kept[s * n : (s + 1) * n] for s in range(dps))
    lane, other = iota((LANES, LANES), 0), iota((LANES, LANES), 1)
    same = (lane // PLANE) == (other // PLANE)
    plane_sums = dot(to_bf16(of_dps), ones_where(same)).astype(jnp.int32)
    need = jnp.max((plane_sums + (dps - 1)) // dps)
    level_ref[0] = sum((need > cap).astype(jnp.int32) for cap in LEVELS)

    at = iota((total, LANES), 0)

    def row_of(values, index):
        return jnp.sum(jnp.where(at == index, values, 0), axis=0, keepdims=True)

    keeps = [row_of(kept, s * n + me) for s in range(dps)]
    eight = iota((8, LANES), 0)
    stacked = to_bf16(sum(jnp.where(eight == s, keeps[s], 0) for s in range(dps)))
    within = dot(stacked, ones_where(same & (lane < other))).astype(jnp.int32)
    whole = dot(stacked, ones_where(same)).astype(jnp.int32)
    bases, starts, base = [], [], jnp.zeros((1, LANES), jnp.int32)
    for s in range(dps):
        bases.append(base)
        starts.append(base + within[s : s + 1])
        base = base + whole[s : s + 1]

    def mine(rows):
        return sum(jnp.where(dp == s, rows[s], 0) for s in range(dps))

    lookup = (
        jnp.where(eight == 0, row_of(ahead_of, dp * n + me), 0)
        + jnp.where(eight == 1, mine(starts), 0)
        + jnp.where(eight == 2, mine(bases), 0)
    ).astype(jnp.float32)
    found = lax.dot_general(
        lookup, named.astype(jnp.float32), (((1,), (0,)), ((), ())),
        precision=lax.Precision.HIGHEST, preferred_element_type=jnp.float32,
    ).astype(jnp.int32)
    slot = found[0:1] + rank
    dealt = found[1:2] + rank
    to, at_row = dealt % dps, dealt // dps
    first = (found[2:3] + (dps - 1) - to) // dps
    place = ids // PLANE * LANES + to * share + at_row - first
    slot_ref[...] = slot
    place_ref[...] = jnp.where(slot < capacity, place, -1)

    row_at, lanes = iota((planes, LANES), 0), iota((planes, LANES), 1)

    def column(values, i):
        return jnp.sum(jnp.where(lanes == row_at * PLANE + i, values, 0), axis=1, keepdims=True)

    merge = jnp.zeros((planes, LANES), jnp.int32)
    meta = jnp.zeros((planes, LANES), jnp.int32)
    used = [jnp.zeros((planes, 1), jnp.int32)] * PLANE
    for s in range(dps):
        begin = (column(bases[s], 0) + (dps - 1) - dp) // dps
        merge = merge + jnp.where(lanes // share == s, begin + lanes % share, 0)
        for i in range(PLANE):
            start, many = column(starts[s], i), column(keeps[s], i)
            begin = (start + (dps - 1) - dp) // dps
            end = (start + many + (dps - 1) - dp) // dps
            inside = (lanes >= begin) & (lanes < end)
            meta = meta + jnp.where(inside, i * most + used[i] + lanes - begin + 1, 0)
            used[i] = used[i] + end - begin
    for k in range(planes):
        merge_ref[k] = merge[k : k + 1]
        meta_ref[k] = meta[k : k + 1] - 1


def survey(capacity, most, ids):
    n, dps = lax.axis_size("expert"), lax.axis_size("dp")
    planes, tok_rows = n // PLANE, ids.shape[1]
    vmem = pl.BlockSpec(memory_space=pltpu.VMEM)
    return pl.pallas_call(
        functools.partial(survey_kernel, capacity, most),
        out_shape=(
            jax.ShapeDtypeStruct((1, tok_rows), jnp.int32),
            jax.ShapeDtypeStruct((1, tok_rows), jnp.int32),
            jax.ShapeDtypeStruct((planes, 1, LANES), jnp.int32),
            jax.ShapeDtypeStruct((planes, 1, LANES), jnp.int32),
            jax.ShapeDtypeStruct((1,), jnp.int32),
        ),
        in_specs=[vmem],
        out_specs=(vmem,) * 4 + (pl.BlockSpec(memory_space=pltpu.SMEM),),
        scratch_shapes=[
            pltpu.VMEM((1, LANES), jnp.int32),
            pltpu.VMEM((PLANE, 1, LANES), jnp.int32),
            pltpu.VMEM((planes, PLANE, 1, LANES), jnp.int32),
            pltpu.VMEM((dps, planes, PLANE, 1, LANES), jnp.int32),
            pltpu.SemaphoreType.DMA((PLANE,)),
            pltpu.SemaphoreType.DMA((PLANE,)),
            pltpu.SemaphoreType.DMA((planes,)),
            pltpu.SemaphoreType.DMA((planes,)),
            pltpu.SemaphoreType.DMA((dps,)),
            pltpu.SemaphoreType.DMA((dps,)),
        ],
        compiler_params=pltpu.CompilerParams(
            collective_id=0, has_side_effects=True, vmem_limit_bytes=16 * 1024 * 1024
        ),
    )(ids)


def exchange_kernel(
    cap, tokens, place, merge, meta, gate_hbm, up_hbm, down_hbm, back_hbm,
    dealt, mixed_in, bucket, relay, relay_meta, spread, arrived, result, gathered, packed, home,
    gate_v, up_v, down_v,
    w_sem, ysend, yrecv, zsend, zrecv, msend, mrecv, xsend, xrecv, rsend, rrecv, bsend, brecv,
    hsend, hrecv,
):
    me, dp = lax.axis_index("expert"), lax.axis_index("dp")
    n, dps = lax.axis_size("expert"), lax.axis_size("dp")
    planes, most, width = n // PLANE, arrived.shape[2], arrived.shape[3]
    z, p = me // PLANE, me % PLANE
    last = planes - 1
    weights = ((gate_hbm, gate_v), (up_hbm, up_v), (down_hbm, down_v))

    def weight_copy(k):
        src, dst = weights[k]
        return pltpu.make_async_copy(src.at[0], dst, w_sem.at[k])

    for k in range(3):
        weight_copy(k).start()
    greet("expert", [z * PLANE + mate_of(p, i, 1) for i in range(1, PLANE)])
    greet("expert", [(z + k) % planes * PLANE + p for k in range(1, planes)])
    greet("dp", [(dp + k) % dps for k in range(1, dps)])
    pl.semaphore_wait(pltpu.get_barrier_semaphore(), PLANE - 1 + planes - 1 + dps - 1)

    def plane_at(group, sign):
        return (z + sign * offset_of(group, planes) + planes) % planes

    def deal_copy(group, k):
        to = (dp + k) % dps
        return pltpu.make_async_remote_copy(
            src_ref=dealt.at[group, to], dst_ref=mixed_in.at[group, dp],
            send_sem=ysend.at[group * dps + k], recv_sem=yrecv.at[group * dps + k],
            device_id={"dp": to},
        )

    def home_copy(group, k):
        to = (dp + k) % dps
        return pltpu.make_async_remote_copy(
            src_ref=dealt.at[group, to], dst_ref=back_hbm.at[plane_at(group, 1), dp],
            send_sem=hsend.at[group * dps + k], recv_sem=hrecv.at[group * dps + k],
            device_id={"dp": to},
        )

    def own_home(group):
        return pltpu.make_async_copy(
            dealt.at[group, dp], back_hbm.at[plane_at(group, 1), dp], hrecv.at[group * dps]
        )

    def meta_copy(group):
        to = plane_at(group, 1)
        return pltpu.make_async_remote_copy(
            src_ref=meta.at[to], dst_ref=relay_meta.at[group],
            send_sem=msend.at[group], recv_sem=mrecv.at[group],
            device_id={"expert": to * PLANE + p},
        )

    def bucket_copy(group):
        return pltpu.make_async_remote_copy(
            src_ref=bucket.at[group], dst_ref=relay.at[group],
            send_sem=zsend.at[group], recv_sem=zrecv.at[group],
            device_id={"expert": plane_at(group, 1) * PLANE + p},
        )

    def spread_copy(group, inner):
        mate = mate_of(p, inner, 1)
        at = group * PLANE + inner
        return pltpu.make_async_remote_copy(
            src_ref=spread.at[group, mate], dst_ref=arrived.at[group, p],
            send_sem=xsend.at[at], recv_sem=xrecv.at[at],
            device_id={"expert": z * PLANE + mate},
        )

    def gather_copy(group, inner):
        mate = mate_of(p, inner, -1)
        at = group * PLANE + inner
        return pltpu.make_async_remote_copy(
            src_ref=result.at[group, mate], dst_ref=gathered.at[group, p],
            send_sem=rsend.at[at], recv_sem=rrecv.at[at],
            device_id={"expert": z * PLANE + mate},
        )

    def back_copy(group):
        return pltpu.make_async_remote_copy(
            src_ref=packed.at[group], dst_ref=home.at[group],
            send_sem=bsend.at[group], recv_sem=brecv.at[group],
            device_id={"expert": plane_at(group, -1) * PLANE + p},
        )

    def send_meta(group, carry):
        meta_copy(group).start()
        return carry

    lax.fori_loop(0, last, send_meta, 0)
    relay_meta[last] = meta[z]

    def deal(group, carry):
        at = place[...]
        targets = iota((LANES, at.shape[1]), 0) + plane_at(group, 1) * LANES
        rows = dot(ones_where(targets == at), tokens[...])
        dealt[group] = rows.astype(jnp.bfloat16).reshape(dps, LANES // dps, width)
        for k in range(1, dps):
            deal_copy(group, k).start()
        mixed_in[group, dp] = dealt[group, dp]
        return carry

    lax.fori_loop(0, planes, deal, 0)

    def merging(group):
        return ones_where(iota((cap, LANES), 0) == merge[plane_at(group, 1)])

    def pool(group):
        for k in range(1, dps):
            deal_copy(group, k).wait_recv()
        rows = dot(merging(group), mixed_in[group].reshape(LANES, width)).astype(jnp.bfloat16)

        @pl.when(group < last)
        def _():
            bucket[group] = rows
            bucket_copy(group).start()

        @pl.when(group == last)
        def _():
            relay[last] = rows

    def routes(group):
        named = relay_meta[group][:, 0:cap]
        return ones_where(iota((PLANE * most, cap), 0) == named)

    def scatter(group):
        @pl.when(group < last)
        def _():
            meta_copy(group).wait_recv()
            bucket_copy(group).wait_recv()

        rows = dot(routes(group), relay[group])
        spread[group] = rows.astype(jnp.bfloat16).reshape(PLANE, most, width)

        def send(inner, carry):
            spread_copy(group, inner).start()
            return carry

        lax.fori_loop(1, PLANE, send, 0)
        arrived[group, p] = spread[group, p]

    def ffn(group):
        def arrive(inner, carry):
            spread_copy(group, inner).wait_recv()
            return carry

        lax.fori_loop(1, PLANE, arrive, 0)
        rows = arrived[group].reshape(PLANE * most, width)
        gate_val = dot(rows, gate_v[...])
        up_val = dot(rows, up_v[...])
        hidden = (jax.nn.silu(gate_val) * up_val).astype(jnp.bfloat16)
        mixed = dot(hidden, down_v[...])
        result[group] = mixed.astype(jnp.bfloat16).reshape(PLANE, most, width)

        def send(inner, carry):
            gather_copy(group, inner).start()
            return carry

        lax.fori_loop(1, PLANE, send, 0)
        gathered[group, p] = result[group, p]

    def give_back(group):
        def arrive(inner, carry):
            gather_copy(group, inner).wait_recv()
            return carry

        lax.fori_loop(1, PLANE, arrive, 0)
        rows = gathered[group].reshape(PLANE * most, width)
        rows = dot(routes(group), rows, ((0,), (0,))).astype(jnp.bfloat16)

        @pl.when(group < last)
        def _():
            packed[group] = rows
            back_copy(group).start()

        @pl.when(group == last)
        def _():
            home[last] = rows

    def step(i, carry):
        @pl.when(i < planes)
        def _():
            pool(i)

        @pl.when(i == LAG)
        def _():
            for k in range(3):
                weight_copy(k).wait()

        @pl.when((i >= LAG) & (i < planes + LAG))
        def _():
            scatter(i - LAG)

        @pl.when((i >= LAG + 1) & (i < planes + LAG + 1))
        def _():
            ffn(i - LAG - 1)

        @pl.when(i >= LAG + 2)
        def _():
            give_back(i - LAG - 2)

        return carry

    lax.fori_loop(0, planes + LAG + 2, step, 0)

    def sent_deals(group, carry):
        for k in range(1, dps):
            deal_copy(group, k).wait_send()
        return carry

    lax.fori_loop(0, planes, sent_deals, 0)

    def go_home(i, carry):
        group = (i + last) % planes

        @pl.when(group < last)
        def _():
            back_copy(group).wait_recv()

        rows = dot(merging(group), home[group], ((0,), (0,)))
        dealt[group] = rows.astype(jnp.bfloat16).reshape(dps, LANES // dps, width)
        for k in range(1, dps):
            home_copy(group, k).start()
        own_home(group).start()
        return carry

    lax.fori_loop(0, planes, go_home, 0)

    def finish_near(at, carry):
        group, inner = at // (PLANE - 1), at % (PLANE - 1) + 1
        spread_copy(group, inner).wait_send()
        gather_copy(group, inner).wait_send()
        return carry

    def finish_far(group, carry):
        meta_copy(group).wait_send()
        bucket_copy(group).wait_send()
        back_copy(group).wait_send()
        return carry

    def finish_home(group, carry):
        own_home(group).wait()
        for k in range(1, dps):
            home_copy(group, k).wait()
        return carry

    lax.fori_loop(0, planes * (PLANE - 1), finish_near, 0)
    lax.fori_loop(0, last, finish_far, 0)
    lax.fori_loop(0, planes, finish_home, 0)


def exchange(level, cap, most, tokens, place, merge, meta, gate_proj, up_proj, down_proj):
    planes, width = merge.shape[0], tokens.shape[1]
    dps, hidden = lax.axis_size("dp"), gate_proj.shape[2]
    vmem, hbm = pl.BlockSpec(memory_space=pltpu.VMEM), pl.BlockSpec(memory_space=pl.ANY)
    blocks = pltpu.VMEM((planes, PLANE, most, width), jnp.bfloat16)
    shares = (planes, dps, LANES // dps, width)
    bucket = pltpu.VMEM((planes, cap, width), jnp.bfloat16)
    of_planes = pltpu.SemaphoreType.DMA((planes,))
    of_dps = pltpu.SemaphoreType.DMA((planes * dps,))
    of_plane = pltpu.SemaphoreType.DMA((planes * PLANE,))
    return pl.pallas_call(
        functools.partial(exchange_kernel, cap),
        out_shape=jax.ShapeDtypeStruct(shares, jnp.bfloat16),
        in_specs=[vmem] * 4 + [hbm] * 3,
        out_specs=hbm,
        scratch_shapes=[
            pltpu.VMEM(shares, jnp.bfloat16),
            pltpu.VMEM(shares, jnp.bfloat16),
            bucket,
            bucket,
            pltpu.VMEM((planes, 1, LANES), jnp.int32),
            blocks,
            blocks,
            blocks,
            blocks,
            bucket,
            bucket,
            pltpu.VMEM((width, hidden), jnp.bfloat16),
            pltpu.VMEM((width, hidden), jnp.bfloat16),
            pltpu.VMEM((hidden, width), jnp.bfloat16),
            pltpu.SemaphoreType.DMA((3,)),
            of_dps, of_dps,
            of_planes, of_planes, of_planes, of_planes,
            of_plane, of_plane, of_plane, of_plane,
            of_planes, of_planes,
            of_dps, of_dps,
        ],
        compiler_params=pltpu.CompilerParams(
            collective_id=1 + level, has_side_effects=True, vmem_limit_bytes=58 * 1024 * 1024
        ),
    )(tokens, place, merge, meta, gate_proj, up_proj, down_proj)


def on_device(tokens, expert_ids, gate_proj, up_proj, down_proj):
    tok_rows, width = tokens.shape
    most = 2 * tok_rows // lax.axis_size("expert")
    capacity = tok_rows * lax.axis_size("dp")
    place, slot, merge, meta, level = survey(capacity, most, expert_ids.reshape(1, tok_rows))

    def at_capacity(level, cap):
        return lambda *operands: exchange(level, cap, most, *operands)

    caps = LEVELS + (PLANE * most,)
    back = lax.switch(
        level[0],
        [at_capacity(k, cap) for k, cap in enumerate(caps)],
        tokens, place, merge, meta, gate_proj, up_proj, down_proj,
    ).reshape(-1, width)
    targets = jnp.arange(back.shape[0], dtype=jnp.int32)
    dispatch = (targets[:, None] == place).astype(jnp.bfloat16)
    mixed = lax.dot_general(
        dispatch, back, (((0,), (0,)), ((), ())), preferred_element_type=jnp.float32
    )
    return (mixed.astype(jnp.bfloat16), slot.reshape(tok_rows))


def solution(mesh):
    in_specs = (
        P(("dp", "expert"), None),
        P(("dp", "expert"), None),
        P("expert", None, None),
        P("expert", None, None),
        P("expert", None, None),
    )
    out_specs = (P(("dp", "expert"), None), P(("dp", "expert")))
    return jax.shard_map(
        on_device, mesh=mesh, in_specs=in_specs, out_specs=out_specs, check_vma=False
    )
```

time: 185 us -> 219 us (1.18)
  the two profiles are of different devices: /device:TPU:1 before, /device:TPU:99 now
where the time goes in v3:
time: 219 us; the launch traced here: 217 us
  Pallas kernels  209 us (95%)
  matrix products  5.91 us (3%)
    pallas_call x1, Pallas kernels, exchange(): pl.pallas_call(functools.partial(exchange_kernel, cap), out_shape=jax.Sha...  191 us
    pallas_call x1, Pallas kernels, survey(): pl.pallas_call(functools.partial(survey_kernel, capacity, most), out_shap...  17.6 us
    dot_general x1, matrix products, on_device(): lax.dot_general(dispatch, back, (((0,), (0,)), ((), ())), preferred_eleme...  5.91 us

profile of v3, /device:TPU:99, one launch (start us, length us, event | category | flops | bytes accessed | tf_op | source)
XLA Modules:
  0.0 217.2 jit_solution(8637999774363096065)
XLA Ops:
  0.6 0.0 copy-start
  0.6 0.7 copy-done
  1.3 17.6 %shard_map.68 = (s32[1,512]{1,0:T(1,128)S(1)}, s32[1,512]{1,0:T(1,128)S(1)}, s32[8,1,128]{2,1,0:T(1,128)S(1)}, s32[8,1,128]{2,1,0:T(1,128)S(1)}, s32[1]{0:T(128)}) custom-call(s32[1,512]{1,0:T(1,128)S(1)} %bitcast.10), custom_call_target="tpu_custom_call" | custom-call | tf_op jit(solution)/shard_map/pallas_call | solution.py:184
  19.5 191.2 %conditional.1 = (bf16[1024,2048]{1,0:T(8,128)(2,1)}) conditional(s32[]{:T(128)} %bitcast.7, (bf16[512,2048]{1,0:T(8,128)(2,1)}, s32[1,512]{1,0:T(1,128)S(1)}, s32[8,1,128]{2,1,0:T(1,128)S(1)}, s32[8,1,128]{2,1,0:T(1,128)S(1)}, bf16[1,2048,768]{2,1,0:T(8,128)(2,1)}, /*index=5*/bf16[1,2048,768]{2,1,0:T(8,128)(2,1)}, ...), branch_computations={%region_0.0_spmd, %region_1.0_spmd, %region_2.0_spmd, %region_3.0_... | conditional | bytes 8 | solution.py:521
  19.5 190.9 %branch_1_fun.1 = bf16[8,4,32,2048]{3,2,1,0:T(8,128)(2,1)} custom-call(bf16[512,2048]{1,0:T(8,128)(2,1)} %get-tuple-element.84.tokens, s32[1,512]{1,0:T(1,128)S(1)} %get-tuple-element.85.place, s32[8,1,128]{2,1,0:T(1,128)S(1)} %get-tuple-element.86.merge, s32[8,1,128]{2,1,0:T(1,128)S(1)} %get-tuple-element.87.meta, ...), custom_call_target="tpu_custom_call" | custom-call | tf_op jit(solution)/shard_map/cond/branch_1_fun/pallas_call | solution.py:478
  210.7 5.9 %convolution_convert_fusion = bf16[512,2048]{1,0:T(8,128)(2,1)} fusion(bf16[1024,2048]{1,0:T(8,128)(2,1)} %get-tuple-element.128, s32[512]{0:T(512)S(1)} %bitcast.17), kind=kOutput, calls=%fused_computation | convolution fusion | flops 2149056512 | bytes 6293504 | tf_op jit(solution)/shard_map/dot_general | solution.py:528
  216.6 0.6 copy.13
Async XLA Ops:
  0.6 0.7 copy-start

commit v4 on v3

--- a/solution.py
+++ b/solution.py
@@ -10,8 +10,9 @@
 NX, NC = 4, 2
 PLANE = NX * NC
 LANES = 128
-LEVELS = (64, 72, 80, 96)
-LAG = 3
+LEVELS = ((72, 24), (80, 24), (80, 32), (128, 32))
+ORDER, HANDLED, OWN = (2, 0, 6, 4, 3, 5, 1, 7), (1, 1, 0, 2, 3, 4, 5, 6, 7), 1
+HOLE, AHEAD, HOME_LAG = 1, 3, 7
 
 
 def mate_of(p, inner, sign):
@@ -21,10 +22,9 @@
     return x * NC + c
 
 
-def offset_of(group, planes):
-    back = planes - 1 - group
-    half, odd = (back + 1) // 2, back % 2
-    return (odd * half + (1 - odd) * (planes - half)) % planes
+def entry(table, i):
+    n = len(table)
+    return table[0] + sum((table[k] - table[k - 1]) * ((i + n - k) // n) for k in range(1, n))
 
 
 def greet(axis, peers):
@@ -111,12 +111,24 @@
     lower = ones_where(iota((total, total), 1) < iota((total, total), 0))
     ahead_of = dot(lower, to_bf16(table)).astype(jnp.int32)
     kept = jnp.clip(capacity - ahead_of, 0, table)
-    of_dps = sum(kept[s * n : (s + 1) * n] for s in range(dps))
     lane, other = iota((LANES, LANES), 0), iota((LANES, LANES), 1)
     same = (lane // PLANE) == (other // PLANE)
-    plane_sums = dot(to_bf16(of_dps), ones_where(same)).astype(jnp.int32)
-    need = jnp.max((plane_sums + (dps - 1)) // dps)
-    level_ref[0] = sum((need > cap).astype(jnp.int32) for cap in LEVELS)
+    plane_sums = dot(to_bf16(kept), ones_where(same)).astype(jnp.int32)
+
+    def largest(values):
+        return jnp.max((values + (dps - 1)) // dps)
+
+    def of_dps(values):
+        return sum(values[s * n : (s + 1) * n] for s in range(dps))
+
+    needs = (
+        largest(of_dps(plane_sums)),
+        largest(plane_sums),
+    )
+    level_ref[0] = sum(
+        functools.reduce(jnp.logical_or, [need > cap for need, cap in zip(needs, caps)]).astype(jnp.int32)
+        for caps in LEVELS[:-1]
+    )
 
     at = iota((total, LANES), 0)
 
@@ -211,7 +223,7 @@
 
 
 def exchange_kernel(
-    cap, tokens, place, merge, meta, gate_hbm, up_hbm, down_hbm, back_hbm,
+    caps, tokens, place, merge, meta, gate_hbm, up_hbm, down_hbm, back_hbm,
     dealt, mixed_in, bucket, relay, relay_meta, spread, arrived, result, gathered, packed, home,
     gate_v, up_v, down_v,
     w_sem, ysend, yrecv, zsend, zrecv, msend, mrecv, xsend, xrecv, rsend, rrecv, bsend, brecv,
@@ -221,7 +233,8 @@
     n, dps = lax.axis_size("expert"), lax.axis_size("dp")
     planes, most, width = n // PLANE, arrived.shape[2], arrived.shape[3]
     z, p = me // PLANE, me % PLANE
-    last = planes - 1
+    cap, share = caps
+    some = pl.ds(0, share)
     weights = ((gate_hbm, gate_v), (up_hbm, up_v), (down_hbm, down_v))
 
     def weight_copy(k):
@@ -230,18 +243,24 @@
 
     for k in range(3):
         weight_copy(k).start()
+
+    def clear(group, carry):
+        mixed_in[group] = jnp.zeros(mixed_in.shape[1:], mixed_in.dtype)
+        return carry
+
+    lax.fori_loop(0, planes, clear, 0)
     greet("expert", [z * PLANE + mate_of(p, i, 1) for i in range(1, PLANE)])
     greet("expert", [(z + k) % planes * PLANE + p for k in range(1, planes)])
     greet("dp", [(dp + k) % dps for k in range(1, dps)])
     pl.semaphore_wait(pltpu.get_barrier_semaphore(), PLANE - 1 + planes - 1 + dps - 1)
 
     def plane_at(group, sign):
-        return (z + sign * offset_of(group, planes) + planes) % planes
+        return (z + sign * entry(ORDER, group) + planes) % planes
 
     def deal_copy(group, k):
         to = (dp + k) % dps
         return pltpu.make_async_remote_copy(
-            src_ref=dealt.at[group, to], dst_ref=mixed_in.at[group, dp],
+            src_ref=dealt.at[group, to, some], dst_ref=mixed_in.at[group, dp, some],
             send_sem=ysend.at[group * dps + k], recv_sem=yrecv.at[group * dps + k],
             device_id={"dp": to},
         )
@@ -249,14 +268,14 @@
     def home_copy(group, k):
         to = (dp + k) % dps
         return pltpu.make_async_remote_copy(
-            src_ref=dealt.at[group, to], dst_ref=back_hbm.at[plane_at(group, 1), dp],
+            src_ref=dealt.at[group, to, some], dst_ref=back_hbm.at[plane_at(group, 1), dp],
             send_sem=hsend.at[group * dps + k], recv_sem=hrecv.at[group * dps + k],
             device_id={"dp": to},
         )
 
     def own_home(group):
         return pltpu.make_async_copy(
-            dealt.at[group, dp], back_hbm.at[plane_at(group, 1), dp], hrecv.at[group * dps]
+            dealt.at[group, dp, some], back_hbm.at[plane_at(group, 1), dp], hrecv.at[group * dps]
         )
 
     def meta_copy(group):
@@ -300,11 +319,14 @@
         )
 
     def send_meta(group, carry):
-        meta_copy(group).start()
-        return carry
-
-    lax.fori_loop(0, last, send_meta, 0)
-    relay_meta[last] = meta[z]
+        @pl.when(group != OWN)
+        def _():
+            meta_copy(group).start()
+
+        return carry
+
+    lax.fori_loop(0, planes, send_meta, 0)
+    relay_meta[OWN] = meta[z]
 
     def deal(group, carry):
         at = place[...]
@@ -316,7 +338,7 @@
         mixed_in[group, dp] = dealt[group, dp]
         return carry
 
-    lax.fori_loop(0, planes, deal, 0)
+    lax.fori_loop(0, AHEAD, deal, 0)
 
     def merging(group):
         return ones_where(iota((cap, LANES), 0) == merge[plane_at(group, 1)])
@@ -326,21 +348,21 @@
             deal_copy(group, k).wait_recv()
         rows = dot(merging(group), mixed_in[group].reshape(LANES, width)).astype(jnp.bfloat16)
 
-        @pl.when(group < last)
+        @pl.when(group != OWN)
         def _():
             bucket[group] = rows
             bucket_copy(group).start()
 
-        @pl.when(group == last)
-        def _():
-            relay[last] = rows
+        @pl.when(group == OWN)
+        def _():
+            relay[OWN] = rows
 
     def routes(group):
         named = relay_meta[group][:, 0:cap]
         return ones_where(iota((PLANE * most, cap), 0) == named)
 
     def scatter(group):
-        @pl.when(group < last)
+        @pl.when(group != OWN)
         def _():
             meta_copy(group).wait_recv()
             bucket_copy(group).wait_recv()
@@ -384,52 +406,50 @@
         rows = gathered[group].reshape(PLANE * most, width)
         rows = dot(routes(group), rows, ((0,), (0,))).astype(jnp.bfloat16)
 
-        @pl.when(group < last)
+        @pl.when(group != OWN)
         def _():
             packed[group] = rows
             back_copy(group).start()
 
-        @pl.when(group == last)
-        def _():
-            home[last] = rows
+        @pl.when(group == OWN)
+        def _():
+            home[OWN] = rows
+
+    def stage(run, at):
+        @pl.when((at >= 0) & (at < len(HANDLED)) & (at != HOLE))
+        def _():
+            run(entry(HANDLED, at))
+
+    def homeward(at):
+        @pl.when((at >= 0) & (at < planes))
+        def _():
+            go_home(entry(HANDLED[:HOLE] + HANDLED[HOLE + 1 :], at))
 
     def step(i, carry):
         @pl.when(i < planes)
         def _():
             pool(i)
 
-        @pl.when(i == LAG)
+        @pl.when(i + AHEAD < planes)
+        def _():
+            deal(i + AHEAD, 0)
+
+        @pl.when(i == 1)
         def _():
             for k in range(3):
                 weight_copy(k).wait()
 
-        @pl.when((i >= LAG) & (i < planes + LAG))
-        def _():
-            scatter(i - LAG)
-
-        @pl.when((i >= LAG + 1) & (i < planes + LAG + 1))
-        def _():
-            ffn(i - LAG - 1)
-
-        @pl.when(i >= LAG + 2)
-        def _():
-            give_back(i - LAG - 2)
-
-        return carry
-
-    lax.fori_loop(0, planes + LAG + 2, step, 0)
-
-    def sent_deals(group, carry):
+        stage(scatter, i - 1)
+        stage(ffn, i - 2)
+        stage(give_back, i - 3)
+        homeward(i - HOME_LAG)
+        return carry
+
+    def go_home(group):
         for k in range(1, dps):
             deal_copy(group, k).wait_send()
-        return carry
-
-    lax.fori_loop(0, planes, sent_deals, 0)
-
-    def go_home(i, carry):
-        group = (i + last) % planes
-
-        @pl.when(group < last)
+
+        @pl.when(group != OWN)
         def _():
             back_copy(group).wait_recv()
 
@@ -438,9 +458,8 @@
         for k in range(1, dps):
             home_copy(group, k).start()
         own_home(group).start()
-        return carry
-
-    lax.fori_loop(0, planes, go_home, 0)
+
+    lax.fori_loop(0, planes + HOME_LAG, step, 0)
 
     def finish_near(at, carry):
         group, inner = at // (PLANE - 1), at % (PLANE - 1) + 1
@@ -449,9 +468,12 @@
         return carry
 
     def finish_far(group, carry):
-        meta_copy(group).wait_send()
-        bucket_copy(group).wait_send()
-        back_copy(group).wait_send()
+        @pl.when(group != OWN)
+        def _():
+            meta_copy(group).wait_send()
+            bucket_copy(group).wait_send()
+            back_copy(group).wait_send()
+
         return carry
 
     def finish_home(group, carry):
@@ -461,23 +483,23 @@
         return carry
 
     lax.fori_loop(0, planes * (PLANE - 1), finish_near, 0)
-    lax.fori_loop(0, last, finish_far, 0)
+    lax.fori_loop(0, planes, finish_far, 0)
     lax.fori_loop(0, planes, finish_home, 0)
 
 
-def exchange(level, cap, most, tokens, place, merge, meta, gate_proj, up_proj, down_proj):
+def exchange(level, caps, most, tokens, place, merge, meta, gate_proj, up_proj, down_proj):
     planes, width = merge.shape[0], tokens.shape[1]
     dps, hidden = lax.axis_size("dp"), gate_proj.shape[2]
     vmem, hbm = pl.BlockSpec(memory_space=pltpu.VMEM), pl.BlockSpec(memory_space=pl.ANY)
     blocks = pltpu.VMEM((planes, PLANE, most, width), jnp.bfloat16)
     shares = (planes, dps, LANES // dps, width)
-    bucket = pltpu.VMEM((planes, cap, width), jnp.bfloat16)
+    bucket = pltpu.VMEM((planes, caps[0], width), jnp.bfloat16)
     of_planes = pltpu.SemaphoreType.DMA((planes,))
     of_dps = pltpu.SemaphoreType.DMA((planes * dps,))
     of_plane = pltpu.SemaphoreType.DMA((planes * PLANE,))
     return pl.pallas_call(
-        functools.partial(exchange_kernel, cap),
-        out_shape=jax.ShapeDtypeStruct(shares, jnp.bfloat16),
+        functools.partial(exchange_kernel, caps),
+        out_shape=jax.ShapeDtypeStruct((planes, dps, caps[1], width), jnp.bfloat16),
         in_specs=[vmem] * 4 + [hbm] * 3,
         out_specs=hbm,
         scratch_shapes=[
@@ -514,21 +536,27 @@
     capacity = tok_rows * lax.axis_size("dp")
     place, slot, merge, meta, level = survey(capacity, most, expert_ids.reshape(1, tok_rows))
 
-    def at_capacity(level, cap):
-        return lambda *operands: exchange(level, cap, most, *operands)
-
-    caps = LEVELS + (PLANE * most,)
-    back = lax.switch(
+    def at_capacity(level, caps):
+        def run(tokens, place, merge, meta, gate_proj, up_proj, down_proj):
+            back = exchange(level, caps, most, tokens, place, merge, meta, gate_proj, up_proj, down_proj)
+            full = LANES // back.shape[1]
+            rows = jnp.where(place < 0, -1, place // full * caps[1] + place % full)
+            targets = jnp.arange(back.size // width, dtype=jnp.int32)
+            dispatch = lax.optimization_barrier((targets[:, None] == rows).astype(jnp.bfloat16))
+            mixed = lax.dot_general(
+                dispatch, back.reshape(-1, width), (((0,), (0,)), ((), ())),
+                preferred_element_type=jnp.float32,
+            )
+            return mixed.astype(jnp.bfloat16)
+
+        return run
+
+    mixed = lax.switch(
         level[0],
-        [at_capacity(k, cap) for k, cap in enumerate(caps)],
+        [at_capacity(k, caps) for k, caps in enumerate(LEVELS)],
         tokens, place, merge, meta, gate_proj, up_proj, down_proj,
-    ).reshape(-1, width)
-    targets = jnp.arange(back.shape[0], dtype=jnp.int32)
-    dispatch = (targets[:, None] == place).astype(jnp.bfloat16)
-    mixed = lax.dot_general(
-        dispatch, back, (((0,), (0,)), ((), ())), preferred_element_type=jnp.float32
     )
-    return (mixed.astype(jnp.bfloat16), slot.reshape(tok_rows))
+    return (mixed, slot.reshape(tok_rows))
 
 
 def solution(mesh):

time: 219 us -> 180 us (0.82)
  Pallas kernels: 209 us -> 171 us
    pallas_call x1, Pallas kernels: 191 us -> 154 us  [exchange(): pl.pallas_call(functools.partial(exchange_kernel, caps), out_shape=jax.Sh...]
where the time goes in v4:
time: 180 us; the launch traced here: 179 us
  Pallas kernels  171 us (95%)
  matrix products  3.74 us (2%)
  local copies, waits for them, and re-layouts  1.99 us (1%)
    pallas_call x1, Pallas kernels, exchange(): pl.pallas_call(functools.partial(exchange_kernel, caps), out_shape=jax.Sh...  154 us
    pallas_call x1, Pallas kernels, survey(): pl.pallas_call(functools.partial(survey_kernel, capacity, most), out_shap...  17.6 us
    dot_general x1, matrix products, run(): lax.dot_general(dispatch, back.reshape(-1, width), (((0,), (0,)), ((), ()...  3.74 us

profile of v4, /device:TPU:99, one launch (start us, length us, event | category | flops | bytes accessed | tf_op | source)
XLA Modules:
  0.0 179.4 jit_solution(8524002437516294857)
XLA Ops:
  0.6 0.0 copy-start
  0.6 0.7 copy-done
  1.3 17.6 %shard_map.68 = (s32[1,512]{1,0:T(1,128)S(1)}, s32[1,512]{1,0:T(1,128)S(1)}, s32[8,1,128]{2,1,0:T(1,128)S(1)}, s32[8,1,128]{2,1,0:T(1,128)S(1)}, s32[1]{0:T(128)}) custom-call(s32[1,512]{1,0:T(1,128)S(1)} %bitcast.19), custom_call_target="tpu_custom_call" | custom-call | tf_op jit(solution)/shard_map/pallas_call | solution.py:196
  19.6 158.5 %conditional.2 = (bf16[512,2048]{1,0:T(8,128)(2,1)S(1)}) conditional(s32[]{:T(128)} %bitcast.9, (s32[1,512]{1,0:T(1,128)S(1)}, bf16[512,2048]{1,0:T(8,128)(2,1)}, s32[8,1,128]{2,1,0:T(1,128)S(1)}, s32[8,1,128]{2,1,0:T(1,128)S(1)}, bf16[1,2048,768]{2,1,0:T(8,128)(2,1)}, /*index=5*/bf16[1,2048,768]{2,1,0:T(8,128)(2,1)}, ...), branch_computations={%region_0.1_spmd, %region_1.2_spmd, %region_2.3_spmd, %region_3.4_... | conditional | flops 2148543488 | bytes 8394760
  19.6 0.3 fusion
  19.9 153.7 %branch_0_fun.1 = bf16[8,4,24,2048]{3,2,1,0:T(8,128)(2,1)} custom-call(bf16[512,2048]{1,0:T(8,128)(2,1)} %get-tuple-element.64.tokens, s32[1,512]{1,0:T(1,128)S(1)} %get-tuple-element.48.place, s32[8,1,128]{2,1,0:T(1,128)S(1)} %get-tuple-element.65.merge, s32[8,1,128]{2,1,0:T(1,128)S(1)} %get-tuple-element.66.meta, ...), custom_call_target="tpu_custom_call" | custom-call | tf_op jit(solution)/shard_map/cond/branch_0_fun/pallas_call | solution.py:500
  173.6 3.7 %fusion.12 = bf16[512,2048]{1,0:T(8,128)(2,1)S(1)} fusion(bf16[768,512]{1,0:T(8,128)(2,1)S(1)} %fusion, bf16[768,2048]{1,0:T(8,128)(2,1)} %bitcast.21), kind=kOutput, calls=%fused_computation.36 | convolution fusion | flops 1610612736 | bytes 6029312 | tf_op jit(solution)/shard_map/cond/branch_0_fun/dot_general | solution.py:546
  178.1 0.0 copy-start.1
  178.1 0.6 copy.12
  178.7 0.7 copy-done.1
  (1 shorter events, 0.0 us)
Async XLA Ops:
  0.6 0.7 copy-start
  178.1 1.3 copy-start.1
